TPU v7x, 256 devices: a 2x2x32 block of a 4x8x32 slice. The times are simulated.
256 devices in a mesh: sample: 4 (over y, x), gz: 64 (over z, core).
Axes of the slice: x: 2, y: 2, z: 32, core: 2. Of those that a mesh axis runs over, the one named last changes fastest.
The devices are a block of a 4x8x32 slice.
Arguments:
- spin_field: float32 [128, 96, 3, 1024], P('gz', 'sample'), parts along dimension 1, may hold values from -1 to 1, as said below
- couplings: int32 [128, 12, 1024], P('gz', 'sample'), parts along dimension 1, may hold values from 0 to 1
- parity_order: int32 [12], P('sample'), parts along dimension 0, may hold values from 0 to 1
- accept: int32 [92], P('sample'), parts along dimension 0, may hold values from 0 to 1
Outputs:
- new_spins: float32 [128, 96, 3, 1024], P('gz', 'sample'), parts along dimension 1
- energies: float32 [96], P('sample'), parts along dimension 0
There are 4 independent parts, one for each index of `sample`. A program takes and returns all parts, laid end to end along the dimension named above; each array names one. Nothing has to cross between parts.
Inputs may be any that keep to these rules, and one draw needn't show every extreme that they name: `spin_field`: every site's spin has unit length.
All inputs are finite; a program needn't handle non-finite values.
Results may differ from a plain program's by a relative error of at most 0.00018.
Values sent between devices are 32-bit elements; how exact they have to be, the bound alone decides.
A program may use at most 64 MiB of HBM per device.

v0:
```python
import functools
import math

import jax
import jax.numpy as jnp
from jax import lax
from jax.experimental import pallas as pl
from jax.experimental.pallas import tpu as pltpu
from jax.sharding import PartitionSpec as P

NY = 32
SWEEPS = 3
STEPS = 2 * SWEEPS
LANES = 128
GROUP = 8
TILE = LANES // NY


def kernel(
    n,
    x_hbm,
    c_hbm,
    par_ref,
    acc_ref,
    out_hbm,
    energy_ref,
    xin,
    cpl,
    coef,
    jz,
    hist,
    part,
    sendbuf,
    recvbuf,
    outv,
    rows,
    gathered,
    apad,
    qs,
    in_sem,
    c_sem,
    out_sem,
    send_sem,
    recv_sem,
    know_sem,
    pair_sem,
    far_send,
    far_recv,
):
    _, comps, replicas, sites = x_hbm.shape
    groups = replicas // GROUP
    tiles = sites // LANES
    half = tiles // 2
    chips = n // 2
    me = lax.axis_index("gz")
    up, down = lax.rem(me + 1, n), lax.rem(me + n - 1, n)
    doublings = [1 << i for i in range(20) if (1 << i) <= n // 4]

    barrier = pltpu.get_barrier_semaphore()
    for neighbour in (down, up):
        pl.semaphore_signal(barrier, inc=1, device_id={"gz": neighbour})

    c_copy = pltpu.make_async_copy(c_hbm, cpl, c_sem)
    c_copy.start()
    x_copies = []
    for g in range(groups):
        window = pl.ds(g * GROUP, GROUP)
        x_copies.append(
            pltpu.make_async_copy(x_hbm.at[:, :, window, :], xin.at[:, :, window, :], in_sem.at[g])
        )
        x_copies[-1].start()

    lane = lax.broadcasted_iota(jnp.int32, (GROUP, LANES), 1)
    column = lane & (NY - 1)
    parity = (lax.shift_right_logical(lane, 5) + lane) & 1
    even = parity == 0

    def cut(k):
        return slice(k * LANES, (k + 1) * LANES)

    def rows_of(g):
        start = g * GROUP
        return pl.ds(start if isinstance(start, int) else pl.multiple_of(start, GROUP), GROUP)

    def shift_x(tiles_in):
        ahead = [pltpu.roll(t, LANES - NY, 1) for t in tiles_in]
        behind = [pltpu.roll(t, NY, 1) for t in tiles_in]
        count = len(tiles_in)
        plus = [jnp.where(lane < LANES - NY, ahead[k], ahead[(k + 1) % count]) for k in range(count)]
        minus = [jnp.where(lane >= NY, behind[k], behind[k - 1]) for k in range(count)]
        return plus, minus

    def plus_y(t):
        return jnp.where(column == NY - 1, pltpu.roll(t, NY - 1, 1), pltpu.roll(t, LANES - 1, 1))

    def minus_y(t):
        return jnp.where(column == 0, pltpu.roll(t, LANES - NY + 1, 1), pltpu.roll(t, 1, 1))

    def colour_of(step):
        return (par_ref[step // 2] + step % 2) % 2

    def changed(step):
        sweep = step // 2
        before = par_ref[jnp.maximum(sweep - 1, 0)]
        return (par_ref[sweep] + before) % 2

    def target_slot(step):
        return step + changed(step) * (1 - 2 * (step % 2))

    def near_slot(step):
        return step + 1 - changed(step) * (1 - step % 2)

    def lower_mask(colour):
        return ((parity + colour) & 1) == 0

    def halo_copy(step, g, way):
        return pltpu.make_async_remote_copy(
            src_ref=sendbuf.at[step, g, way],
            dst_ref=recvbuf.at[step, g, way],
            send_sem=send_sem.at[step, g, way],
            recv_sem=recv_sem.at[step, g, way],
            device_id={"gz": up if way == 0 else down},
        )

    def send_halo(step, g):
        mask = lower_mask(colour_of(step))
        slot = near_slot(step)
        for c in range(comps):
            for k in range(half):
                low = hist[slot, c, rows_of(g), cut(k)]
                high = hist[slot, c, rows_of(g), cut(k + half)]
                sendbuf[step, g, 0, c, :, cut(k)] = jnp.where(
                    mask, low * jz[1, :, cut(k)], pltpu.roll(high * jz[1, :, cut(k + half)], NY, 1)
                )
                sendbuf[step, g, 1, c, :, cut(k)] = jnp.where(mask, pltpu.roll(high, NY, 1), low)
        for way in range(2):
            halo_copy(step, g, way).start()

    def local_part(step, g):
        slot = near_slot(step)
        colour = colour_of(step)
        for c in range(comps):
            near = [hist[slot, c, rows_of(g), cut(k)] for k in range(tiles)]
            plus_x, minus_x = shift_x(near)
            for k in range(tiles):
                part[c, rows_of(g), cut(k)] = (
                    coef[colour, 0, :, cut(k)] * plus_x[k]
                    + coef[colour, 1, :, cut(k)] * minus_x[k]
                    + coef[colour, 2, :, cut(k)] * plus_y(near[k])
                    + coef[colour, 3, :, cut(k)] * minus_y(near[k])
                    + jz[0, :, cut(k)] * near[k]
                )

    def update(step, g, last=False):
        mask = lower_mask(colour_of(step))
        slot = target_slot(step)
        for way in range(2):
            halo_copy(step, g, way).wait_recv()
        energy = jnp.zeros((GROUP, LANES), jnp.float32)
        for k in range(half):
            outer = [[], []]
            for c in range(comps):
                from_below = recvbuf[step, g, 0, c, :, cut(k)]
                from_above = recvbuf[step, g, 1, c, :, cut(k)]
                outer[0].append(jnp.where(mask, from_below, from_above * jz[1, :, cut(k)]))
                other = pltpu.roll(jnp.where(mask, from_above, from_below), LANES - NY, 1)
                outer[1].append(jnp.where(mask, other, other * jz[1, :, cut(k + half)]))
            for side in range(2):
                where = cut(k + side * half)
                local = [part[c, rows_of(g), where] + outer[side][c] for c in range(comps)]
                spins = [hist[slot, c, rows_of(g), where] for c in range(comps)]
                along = sum(s * f for s, f in zip(spins, local))
                strength = jnp.maximum(sum(f * f for f in local), 1.0)
                factor = 2.0 * along / strength
                for c in range(comps):
                    new = factor * local[c] - spins[c]
                    hist[step + 2, c, rows_of(g), where] = new
                    if last:
                        energy += new * local[c]
        return energy

    c_copy.wait()
    bonds = []
    for d in range(3):
        bonds.append([])
        for z in range(2):
            signs = (2 * cpl[d, z : z + 1, :] - 1).astype(jnp.float32)
            signs = jnp.broadcast_to(signs, (GROUP, sites))
            bonds[d].append([signs[:, cut(k)] for k in range(tiles)])
    for z in range(2):
        for k in range(tiles):
            jz[z, :, cut(k)] = bonds[2][z][k]

    slot0_mask = lower_mask(par_ref[0])
    for g in range(groups):
        x_copies[g].wait()
        for c in range(comps):
            for k in range(tiles):
                lower = xin[0, c, rows_of(g), cut(k)]
                upper = xin[1, c, rows_of(g), cut(k)]
                hist[0, c, rows_of(g), cut(k)] = jnp.where(slot0_mask, lower, upper)
                hist[1, c, rows_of(g), cut(k)] = jnp.where(slot0_mask, upper, lower)
        if g == 0:
            pl.semaphore_wait(barrier, 2)
        send_halo(0, g)

    def greet(i):
        for way, there in enumerate((lax.rem(me + doublings[i], n), lax.rem(me + n - doublings[i], n))):
            pl.semaphore_signal(know_sem.at[i, way], inc=1, device_id={"gz": there})

    def heard(i):
        for way in range(2):
            pl.semaphore_wait(know_sem.at[i, way], 1)

    greet(0)

    shifted = [[shift_x(bonds[0][z])[1] for z in range(2)], [[minus_y(t) for t in bonds[1][z]] for z in range(2)]]
    for colour in range(2):
        for k in range(tiles):
            for j, signs in enumerate((bonds[0], shifted[0], bonds[1], shifted[1])):
                first, second = (signs[0][k], signs[1][k]) if colour == 0 else (signs[1][k], signs[0][k])
                coef[colour, j, :, cut(k)] = jnp.where(even, first, second)

    for g in range(groups):
        local_part(0, g)

    apad[0] = 0
    for k in range(replicas - 1):
        apad[k + 1] = acc_ref[k]
    apad[replicas] = 0
    accept_next = jnp.zeros((GROUP, LANES), jnp.int32)
    for k in range(replicas - 1):
        accept_next = jnp.where(lane == k, acc_ref[k], accept_next)
    accept_prev = pltpu.roll(accept_next, 1, 1)
    odd_slot = lane & 1
    first_source = lane + jnp.where(odd_slot == 0, accept_next, -accept_prev)
    order = jnp.where(
        odd_slot == 1,
        jnp.where(accept_next == 1, pltpu.roll(first_source, LANES - 1, 1), first_source),
        jnp.where(accept_prev == 1, pltpu.roll(first_source, 1, 1), first_source),
    )
    for t in range(replicas):
        middle = t + apad[t + 1] if t % 2 else t - apad[t]
        odd = middle % 2
        qs[t] = middle + (1 - odd) * apad[middle + 1] - odd * apad[middle]

    def one_step(step, carry):
        def one_group(g, inner):
            update(step, g)
            send_halo(step + 1, g)
            local_part(step + 1, g)
            return inner

        lax.fori_loop(0, groups, one_group, 0)
        for i in range(len(doublings)):
            @pl.when(step == i)
            def _():
                heard(i)
                if i + 1 < len(doublings):
                    greet(i + 1)
        return carry

    lax.fori_loop(0, STEPS - 1, one_step, 0)
    for i in range(STEPS - 1, len(doublings)):
        heard(i)
        if i + 1 < len(doublings):
            greet(i + 1)

    sublane = lax.broadcasted_iota(jnp.int32, (GROUP, LANES), 0)
    spread = jnp.zeros((GROUP, LANES), jnp.float32)
    for g in range(groups):
        energy = update(STEPS - 1, g, last=True)
        total = jnp.sum(energy, axis=1, keepdims=True)
        spread += jnp.where(order == sublane + g * GROUP, total, 0.0)
    rows[0] = jnp.sum(spread, axis=0, keepdims=True)

    chip = me // 2
    partner = me + 1 - 2 * (me % 2)
    pair = pltpu.make_async_remote_copy(
        src_ref=rows.at[0],
        dst_ref=rows.at[1],
        send_sem=pair_sem.at[0],
        recv_sem=pair_sem.at[1],
        device_id={"gz": partner},
    )
    pair.start()
    pair.wait_recv()
    rows[2] = rows[0] + rows[1]

    def far_copy(distance):
        return pltpu.make_async_remote_copy(
            src_ref=rows.at[2],
            dst_ref=gathered.at[chip],
            send_sem=far_send.at[distance],
            recv_sem=far_recv.at[chip],
            device_id={"gz": lax.rem(me + 2 * distance, n)},
        )

    far_first = sorted(range(1, chips), key=lambda d: -min(d, chips - d))
    for distance in far_first:
        far_copy(distance).start()
    gathered[chip] = rows[2]

    row_lane = lax.broadcasted_iota(jnp.int32, (1, sites), 1)
    row_parity = lax.shift_right_logical(row_lane, 5) + row_lane
    final_mask = ((row_parity + par_ref[SWEEPS - 1]) & 1) == 0

    def one_slot(t, carry):
        q = qs[t]
        for c in range(comps):
            first = hist[STEPS, c, pl.ds(q, 1), :]
            second = hist[STEPS + 1, c, pl.ds(q, 1), :]
            outv[0, c, pl.ds(t, 1), :] = jnp.where(final_mask, first, second)
            outv[1, c, pl.ds(t, 1), :] = jnp.where(final_mask, second, first)
        return carry

    lax.fori_loop(0, replicas, one_slot, 0)
    out_copy = pltpu.make_async_copy(outv, out_hbm, out_sem)
    out_copy.start()

    for distance in range(1, chips):
        source = lax.rem(chip + chips - distance, chips)
        pltpu.make_async_remote_copy(
            src_ref=rows.at[2],
            dst_ref=gathered.at[source],
            send_sem=far_send.at[distance],
            recv_sem=far_recv.at[source],
            device_id={"gz": lax.rem(me + 2 * distance, n)},
        ).wait_recv()
    scale = -1.0 / math.sqrt(sites * 2 * n)
    energy_ref[...] = jnp.sum(gathered[...], axis=0) * scale

    out_copy.wait()
    pair.wait_send()
    for distance in range(1, chips):
        far_copy(distance).wait_send()

    def drain(step, carry):
        def drain_group(g, inner):
            for way in range(2):
                halo_copy(step, g, way).wait_send()
            return inner

        return lax.fori_loop(0, groups, drain_group, carry)

    lax.fori_loop(0, STEPS, drain, 0)


def body(spin_field, couplings, parity_order, accept):
    planes, replicas, comps, sites = spin_field.shape
    n = lax.axis_size("gz")
    groups = replicas // GROUP
    chips = n // 2
    levels = max(1, sum(1 for i in range(20) if (1 << i) <= n // 4))
    dma = pltpu.SemaphoreType.DMA
    out, energy = pl.pallas_call(
        functools.partial(kernel, n),
        out_shape=(
            jax.ShapeDtypeStruct((planes, comps, replicas, sites), jnp.float32),
            jax.ShapeDtypeStruct((1, LANES), jnp.float32),
        ),
        in_specs=[
            pl.BlockSpec(memory_space=pl.ANY),
            pl.BlockSpec(memory_space=pl.ANY),
            pl.BlockSpec(memory_space=pltpu.SMEM),
            pl.BlockSpec(memory_space=pltpu.SMEM),
        ],
        out_specs=(pl.BlockSpec(memory_space=pl.ANY), pl.BlockSpec(memory_space=pltpu.VMEM)),
        scratch_shapes=[
            pltpu.VMEM((planes, comps, replicas, sites), jnp.float32),
            pltpu.VMEM((3, planes, sites), jnp.int32),
            pltpu.VMEM((2, 4, GROUP, sites), jnp.float32),
            pltpu.VMEM((2, GROUP, sites), jnp.float32),
            pltpu.VMEM((STEPS + 2, comps, replicas, sites), jnp.float32),
            pltpu.VMEM((comps, replicas, sites), jnp.float32),
            pltpu.VMEM((STEPS, groups, 2, comps, GROUP, sites // 2), jnp.float32),
            pltpu.VMEM((STEPS, groups, 2, comps, GROUP, sites // 2), jnp.float32),
            pltpu.VMEM((planes, comps, replicas, sites), jnp.float32),
            pltpu.VMEM((3, 1, LANES), jnp.float32),
            pltpu.VMEM((chips, 1, LANES), jnp.float32),
            pltpu.SMEM((replicas + 1,), jnp.int32),
            pltpu.SMEM((replicas,), jnp.int32),
            dma((groups,)),
            dma,
            dma,
            dma((STEPS, groups, 2)),
            dma((STEPS, groups, 2)),
            pltpu.SemaphoreType.REGULAR((levels, 2)),
            dma((2,)),
            dma((chips,)),
            dma((chips,)),
        ],
        compiler_params=pltpu.CompilerParams(collective_id=0, has_side_effects=True),
    )(spin_field.transpose(0, 2, 1, 3), couplings.transpose(1, 0, 2), parity_order, accept)
    return out.transpose(0, 2, 1, 3), energy[0, :replicas]


def solution(mesh):
    in_specs = (P("gz", "sample", None, None), P("gz", "sample", None), P("sample"), P("sample"))
    out_specs = (P("gz", "sample", None, None), P("sample"))
    return jax.shard_map(body, mesh=mesh, in_specs=in_specs, out_specs=out_specs, check_vma=False)
```

profile of v0, /device:TPU:37, one launch (start us, length us, event | category | flops | bytes accessed | tf_op | source)
XLA Modules:
  0.0 63.4 jit_solution(15082535690119218055)
XLA Ops:
  0.6 59.7 %shard_map.59 = (f32[2,3,24,1024]{3,2,1,0:T(8,128)}, f32[1,128]{1,0:T(1,128)}) custom-call(f32[2,3,24,1024]{3,2,1,0:T(8,128)} %bitcast.5, s32[3,2,1024]{2,1,0:T(2,128)} %bitcast.7, s32[3]{0:T(128)} %par_ref.1, s32[23]{0:T(128)} %acc_ref.1), custom_call_target="tpu_custom_call" | custom-call | tf_op jit(solution)/shard_map/pallas_call | solution.py:356
  60.3 0.0 copy-start
  60.3 0.7 %copy-done = f32[1,128]{1,0:T(1,128)S(1)} copy-done((f32[1,128]{1,0:T(1,128)S(1)}, f32[1,128]{1,0:T(1,128)}, u32[]{:S(2)}) %copy-start) | copy-done | bytes 536
  61.0 0.5 slice_bitcast_fusion
  61.5 1.9 %copy.7 = f32[2,24,3,1024]{3,1,2,0:T(8,128)} copy(f32[2,24,3,1024]{3,1,2,0:T(8,128)} %bitcast.6) | data formatting | bytes 1179648
Async XLA Ops:
  60.3 0.7 %copy-start = (f32[1,128]{1,0:T(1,128)S(1)}, f32[1,128]{1,0:T(1,128)}, u32[]{:S(2)}) copy-start(f32[1,128]{1,0:T(1,128)} %get-tuple-element.5) | copy-start | bytes 1540
where the time goes:
time: 63.6 us; the launch traced here: 63.4 us
  Pallas kernels  59.7 us (94%)
  local copies, waits for them, and re-layouts  3.09 us (5%)
  between operations  0.65 us (1%)
    pallas_call x1, Pallas kernels, body(): pl.pallas_call(functools.partial(kernel, n), out_shape=(jax.ShapeDtypeStr...  59.7 us
    unnamed x3, local copies, waits for them, and re-layouts  2.58 us

commit v1 on v0

v1 whole, which is shorter than its diff:
```python
import functools
import math

import jax
import jax.numpy as jnp
from jax import lax
from jax.experimental import pallas as pl
from jax.experimental.pallas import tpu as pltpu
from jax.sharding import PartitionSpec as P

NY = 32
SWEEPS = 3
STEPS = 2 * SWEEPS
LANES = 128
TILE = LANES // NY
GROUP = 8
UNITS = 4
NEWS_AT = ((0, 0), (0, 2), (1, 1), (2, 1))


def kernel(
    n,
    x_hbm,
    c_hbm,
    par_hbm,
    acc_hbm,
    out_ref,
    energy_ref,
    xin,
    cpl,
    coef,
    jz,
    hist,
    part,
    sendbuf,
    recvbuf,
    energy_row,
    gathered,
    par_ref,
    acc_ref,
    apad,
    qs,
    in_sem,
    c_sem,
    par_sem,
    acc_sem,
    send_sem,
    recv_sem,
    know_sem,
    far_sem,
):
    _, comps, replicas, sites = x_hbm.shape
    groups = replicas // GROUP
    tiles = sites // LANES
    half = tiles // 2
    pairs = half // UNITS
    me = lax.axis_index("gz")
    up, down = lax.rem(me + 1, n), lax.rem(me + n - 1, n)
    doublings = [1 << i for i in range(20) if (1 << i) <= n // 4]

    barrier = pltpu.get_barrier_semaphore()
    for neighbour in (down, up):
        pl.semaphore_signal(barrier, inc=1, device_id={"gz": neighbour})

    par_copy = pltpu.make_async_copy(par_hbm, par_ref, par_sem)
    par_copy.start()
    c_copy = pltpu.make_async_copy(c_hbm, cpl, c_sem)
    c_copy.start()
    x_copies = []
    for g in range(groups):
        window = pl.ds(g * GROUP, GROUP)
        x_copies.append(
            pltpu.make_async_copy(x_hbm.at[:, :, window, :], xin.at[:, :, window, :], in_sem.at[g])
        )
        x_copies[-1].start()
    acc_copy = pltpu.make_async_copy(acc_hbm, acc_ref, acc_sem)
    acc_copy.start()

    lane = lax.broadcasted_iota(jnp.int32, (GROUP, LANES), 1)
    column = lane & (NY - 1)
    low = lax.broadcasted_iota(jnp.int32, (GROUP, LANES), 0) < GROUP // 2
    plain_parity = (lax.shift_right_logical(lane, 5) + lane) & 1
    row = (lax.shift_right_logical(lane, 5) + jnp.where(low, 0, TILE - 1)) & (TILE - 1)
    parity = (row + lane) & 1
    last_row, first_row = row == TILE - 1, row == 0

    def into_frame(t):
        return jnp.where(low, t, pltpu.roll(t, NY, 1))

    def out_of_frame(t):
        return jnp.where(low, t, pltpu.roll(t, LANES - NY, 1))

    def swap_halves(t):
        return pltpu.roll(t, GROUP // 2, 0)

    def cut(k):
        return slice(k * LANES, (k + 1) * LANES)

    def shift_x(tiles_in):
        ahead = [pltpu.roll(t, LANES - NY, 1) for t in tiles_in]
        behind = [pltpu.roll(t, NY, 1) for t in tiles_in]
        count = len(tiles_in)
        plus = [jnp.where(last_row, ahead[(k + 1) % count], ahead[k]) for k in range(count)]
        minus = [jnp.where(first_row, behind[k - 1], behind[k]) for k in range(count)]
        return plus, minus

    def plus_y(t):
        return jnp.where(column == NY - 1, pltpu.roll(t, NY - 1, 1), pltpu.roll(t, LANES - 1, 1))

    def minus_y(t):
        return jnp.where(column == 0, pltpu.roll(t, LANES - NY + 1, 1), pltpu.roll(t, 1, 1))

    def minus_y_all(tiles_in):
        return [minus_y(t) for t in tiles_in]

    def colour_of(step):
        return (par_ref[step // 2] + step % 2) % 2

    def changed(step):
        sweep = step // 2
        before = par_ref[jnp.maximum(sweep - 1, 0)]
        return (par_ref[sweep] + before) % 2

    def target_slot(step):
        return step + changed(step) * (1 - 2 * (step % 2))

    def near_slot(step):
        return step + 1 - changed(step) * (1 - step % 2)

    def lower_mask(colour):
        return ((parity + colour) & 1) == 0

    def halo_copy(step, g, u, way):
        return pltpu.make_async_remote_copy(
            src_ref=sendbuf.at[step, g, u, way],
            dst_ref=recvbuf.at[step, g, u, way],
            send_sem=send_sem,
            recv_sem=recv_sem.at[step % 2, g, u],
            device_id={"gz": up if way == 0 else down},
        )

    def both_halos(step, g, u):
        return pltpu.make_async_remote_copy(
            src_ref=sendbuf.at[step, g, u],
            dst_ref=recvbuf.at[step, g, u],
            send_sem=send_sem,
            recv_sem=recv_sem.at[step % 2, g, u],
            device_id={"gz": up},
        )

    def fill_halo(step, g, u):
        mask = lower_mask(colour_of(step))
        slot = near_slot(step)
        for p in range(pairs):
            k = u * pairs + p
            for c in range(comps):
                to_above, to_below = [], []
                for tile in (k, k + half):
                    spins = hist[slot, c, g, tile]
                    swapped = swap_halves(spins)
                    to_above.append(jnp.where(mask, spins * jz[1, tile], swapped * jz[2, tile]))
                    to_below.append(jnp.where(mask, swapped, spins))
                sendbuf[step, g, u, 0, c, p] = jnp.where(low, *to_above)
                sendbuf[step, g, u, 1, c, p] = jnp.where(low, *to_below)

    def send_halo(step, g, u):
        for way in range(2):
            halo_copy(step, g, u, way).start()

    def local_part(step, g):
        slot = near_slot(step)
        colour = colour_of(step)
        for c in range(comps):
            near = [hist[slot, c, g, k] for k in range(tiles)]
            plus_x, minus_x = shift_x(near)
            for k in range(tiles):
                part[c, g, k] = (
                    coef[colour, 0, k] * plus_x[k]
                    + coef[colour, 1, k] * minus_x[k]
                    + coef[colour, 2, k] * plus_y(near[k])
                    + coef[colour, 3, k] * minus_y(near[k])
                    + jz[0, k] * near[k]
                )

    def update(step, g, u, energy=None):
        mask = lower_mask(colour_of(step))
        slot = target_slot(step)
        both_halos(step, g, u).wait_recv()
        for p in range(pairs):
            k = u * pairs + p
            outer = [[], []]
            for c in range(comps):
                below, above = recvbuf[step, g, u, 0, c, p], recvbuf[step, g, u, 1, c, p]
                below_swapped, above_swapped = swap_halves(below), swap_halves(above)
                outer[0].append(
                    jnp.where(
                        mask,
                        jnp.where(low, below, below_swapped),
                        jnp.where(low, above, above_swapped) * jz[1, k],
                    )
                )
                outer[1].append(
                    jnp.where(
                        mask,
                        jnp.where(low, below_swapped, below),
                        jnp.where(low, above_swapped, above) * jz[1, k + half],
                    )
                )
            for side in range(2):
                tile = k + side * half
                local = [part[c, g, tile] + outer[side][c] for c in range(comps)]
                spins = [hist[slot, c, g, tile] for c in range(comps)]
                along = sum(s * f for s, f in zip(spins, local))
                strength = jnp.maximum(sum(f * f for f in local), 1.0)
                factor = 2.0 * along / strength
                for c in range(comps):
                    new = factor * local[c] - spins[c]
                    hist[step + 2, c, g, tile] = new
                    if energy is not None:
                        energy += new * local[c]
        return energy

    def signs_of(d, z):
        signs = (2 * cpl[d, z : z + 1, :] - 1).astype(jnp.float32)
        signs = jnp.broadcast_to(signs, (GROUP, sites))
        return [signs[:, cut(k)] for k in range(tiles)]

    c_copy.wait()
    for z in range(2):
        for k, signs in enumerate(signs_of(2, z)):
            jz[z, k] = into_frame(signs)
            if z == 1:
                jz[2, k] = swap_halves(jz[1, k])
    par_copy.wait()
    first_mask = lower_mask(par_ref[0])
    for g in range(groups):
        x_copies[g].wait()
        window = slice(g * GROUP, (g + 1) * GROUP)
        for c in range(comps):
            for k in range(tiles):
                lower = into_frame(xin[0, c, window, cut(k)])
                upper = into_frame(xin[1, c, window, cut(k)])
                hist[0, c, g, k] = jnp.where(first_mask, lower, upper)
                hist[1, c, g, k] = jnp.where(first_mask, upper, lower)
        for u in range(UNITS):
            fill_halo(0, g, u)
            if g == 0 and u == 0:
                pl.semaphore_wait(barrier, 2)
            send_halo(0, g, u)

    def greet(i):
        for there in (lax.rem(me + doublings[i], n), lax.rem(me + n - doublings[i], n)):
            pl.semaphore_signal(know_sem.at[i], inc=1, device_id={"gz": there})

    def pass_on(i):
        pl.semaphore_wait(know_sem.at[i], 2)
        if i + 1 < len(doublings):
            greet(i + 1)

    greet(0)

    for j, (d, shift) in enumerate(((0, lambda t: t), (0, lambda t: shift_x(t)[1]), (1, lambda t: t), (1, minus_y_all))):
        lower, upper = (shift([into_frame(t) for t in signs_of(d, z)]) for z in range(2))
        for k in range(tiles):
            coef[0, j, k] = jnp.where(parity == 0, lower[k], upper[k])
            coef[1, j, k] = jnp.where(parity == 0, upper[k], lower[k])

    for g in range(groups):
        local_part(0, g)

    acc_copy.wait()
    apad[0] = 0
    for k in range(replicas - 1):
        apad[k + 1] = acc_ref[k]
    apad[replicas] = 0
    accept_next = jnp.zeros((GROUP, LANES), jnp.int32)
    for k in range(replicas - 1):
        accept_next = jnp.where(lane == k, acc_ref[k], accept_next)
    accept_prev = pltpu.roll(accept_next, 1, 1)
    odd_slot = lane & 1
    first_source = lane + jnp.where(odd_slot == 0, accept_next, -accept_prev)
    order = jnp.where(
        odd_slot == 1,
        jnp.where(accept_next == 1, pltpu.roll(first_source, LANES - 1, 1), first_source),
        jnp.where(accept_prev == 1, pltpu.roll(first_source, 1, 1), first_source),
    )
    for t in range(replicas):
        middle = t + apad[t + 1] if t % 2 else t - apad[t]
        odd = middle % 2
        qs[t] = middle + (1 - odd) * apad[middle + 1] - odd * apad[middle]

    def one_step(step, carry):
        for g in range(groups):
            for i, (at_step, at_group) in enumerate(NEWS_AT[: len(doublings)]):
                if g == at_group:
                    @pl.when(step == at_step)
                    def _():
                        pass_on(i)
            for u in range(UNITS):
                update(step, g, u)
                fill_halo(step + 1, g, u)
                send_halo(step + 1, g, u)
        for g in range(groups):
            local_part(step + 1, g)
        return carry

    lax.fori_loop(0, STEPS - 1, one_step, 0)

    sublane = lax.broadcasted_iota(jnp.int32, (GROUP, LANES), 0)
    spread = jnp.zeros((GROUP, LANES), jnp.float32)
    for g in range(groups):
        energy = jnp.zeros((GROUP, LANES), jnp.float32)
        for u in range(UNITS):
            energy = update(STEPS - 1, g, u, energy)
        total = jnp.sum(energy, axis=1, keepdims=True)
        spread += jnp.where(order == sublane + g * GROUP, total, 0.0)
    energy_row[...] = jnp.sum(spread, axis=0, keepdims=True)

    for i in range(len(NEWS_AT), len(doublings)):
        pass_on(i)

    def far_copy(distance):
        return pltpu.make_async_remote_copy(
            src_ref=energy_row,
            dst_ref=gathered.at[me],
            send_sem=far_sem.at[0],
            recv_sem=far_sem.at[1],
            device_id={"gz": lax.rem(me + distance, n)},
        )

    for distance in sorted(range(1, n), key=lambda d: abs(2 * d - n)):
        far_copy(distance).start()
    gathered[me] = energy_row[...]

    final_mask = ((plain_parity + par_ref[SWEEPS - 1]) & 1) == 0
    for g in range(groups):
        window = slice(g * GROUP, (g + 1) * GROUP)
        for c in range(comps):
            for k in range(tiles):
                first = out_of_frame(hist[STEPS, c, g, k])
                second = out_of_frame(hist[STEPS + 1, c, g, k])
                xin[0, c, window, cut(k)] = jnp.where(final_mask, first, second)
                xin[1, c, window, cut(k)] = jnp.where(final_mask, second, first)

    def one_slot(t, carry):
        for z in range(2):
            for c in range(comps):
                out_ref[z, c, pl.ds(t, 1), :] = xin[z, c, pl.ds(qs[t], 1), :]
        return carry

    lax.fori_loop(0, replicas, one_slot, 0)

    pltpu.make_async_remote_copy(
        src_ref=sendbuf,
        dst_ref=recvbuf,
        send_sem=send_sem,
        recv_sem=recv_sem.at[0, 0, 0],
        device_id={"gz": up},
    ).wait_send()
    others = gathered.at[pl.ds(0, n - 1)]
    all_far = pltpu.make_async_remote_copy(
        src_ref=others,
        dst_ref=others,
        send_sem=far_sem.at[0],
        recv_sem=far_sem.at[1],
        device_id={"gz": up},
    )
    all_far.wait_send()
    all_far.wait_recv()
    scale = -1.0 / math.sqrt(sites * 2 * n)
    energy_ref[...] = jnp.sum(gathered[...], axis=0) * scale


def body(spin_field, couplings, parity_order, accept):
    planes, replicas, comps, sites = spin_field.shape
    n = lax.axis_size("gz")
    groups = replicas // GROUP
    tiles = sites // LANES
    levels = max(1, sum(1 for i in range(20) if (1 << i) <= n // 4))
    dma = pltpu.SemaphoreType.DMA
    halo = (STEPS, groups, UNITS, 2)
    tile = (GROUP, LANES)
    anywhere = pl.BlockSpec(memory_space=pl.ANY)
    vmem = pl.BlockSpec(memory_space=pltpu.VMEM)
    out, energy = pl.pallas_call(
        functools.partial(kernel, n),
        out_shape=(
            pltpu.VMEM((planes, comps, replicas, sites), jnp.float32),
            pltpu.VMEM((1, LANES), jnp.float32),
        ),
        in_specs=[anywhere] * 4,
        out_specs=(vmem, vmem),
        scratch_shapes=[
            pltpu.VMEM((planes, comps, replicas, sites), jnp.float32),
            pltpu.VMEM((3, planes, sites), jnp.int32),
            pltpu.VMEM((2, 4, tiles, *tile), jnp.float32),
            pltpu.VMEM((3, tiles, *tile), jnp.float32),
            pltpu.VMEM((STEPS + 2, comps, groups, tiles, *tile), jnp.float32),
            pltpu.VMEM((comps, groups, tiles, *tile), jnp.float32),
            pltpu.VMEM((*halo, comps, tiles // 2 // UNITS, *tile), jnp.float32),
            pltpu.VMEM((*halo, comps, tiles // 2 // UNITS, *tile), jnp.float32),
            pltpu.VMEM((1, LANES), jnp.float32),
            pltpu.VMEM((n, 1, LANES), jnp.float32),
            pltpu.SMEM(parity_order.shape, jnp.int32),
            pltpu.SMEM(accept.shape, jnp.int32),
            pltpu.SMEM((replicas + 1,), jnp.int32),
            pltpu.SMEM((replicas,), jnp.int32),
            dma((groups,)),
            dma,
            dma,
            dma,
            dma,
            dma((2, groups, UNITS)),
            pltpu.SemaphoreType.REGULAR((levels,)),
            dma((2,)),
        ],
        compiler_params=pltpu.CompilerParams(collective_id=0, has_side_effects=True),
    )(spin_field.transpose(0, 2, 1, 3), couplings.transpose(1, 0, 2), parity_order, accept)
    return out.transpose(0, 2, 1, 3), energy[0, :replicas]


def solution(mesh):
    in_specs = (P("gz", "sample", None, None), P("gz", "sample", None), P("sample"), P("sample"))
    out_specs = (P("gz", "sample", None, None), P("sample"))
    return jax.shard_map(body, mesh=mesh, in_specs=in_specs, out_specs=out_specs, check_vma=False)
```

time: 63.6 us -> 55.7 us (0.88)
  Pallas kernels: 59.7 us -> 53.6 us
  local copies, waits for them, and re-layouts: 3.09 us -> 1.33 us
    pallas_call x1, Pallas kernels: 59.7 us -> 53.6 us  [body(): pl.pallas_call(functools.partial(kernel, n), out_shape=(pltpu.VMEM((plane...]
    unnamed x3 -> x1, local copies, waits for them, and re-layouts: 2.58 us -> 0.82 us
where the time goes in v1:
time: 55.7 us; the launch traced here: 55.6 us
  Pallas kernels  53.6 us (96%)
  local copies, waits for them, and re-layouts  1.33 us (2%)
  between operations  0.64 us (1%)
    pallas_call x1, Pallas kernels, body(): pl.pallas_call(functools.partial(kernel, n), out_shape=(pltpu.VMEM((plane...  53.6 us

profile of v1, /device:TPU:37, one launch (start us, length us, event | category | flops | bytes accessed | tf_op | source)
XLA Modules:
  0.0 55.6 jit_solution(11908794898798690702)
XLA Ops:
  0.6 53.6 %shard_map.59 = (f32[2,3,24,1024]{3,2,1,0:T(8,128)S(1)}, f32[1,128]{1,0:T(1,128)S(1)}) custom-call(f32[2,3,24,1024]{3,2,1,0:T(8,128)} %bitcast.6, s32[3,2,1024]{2,1,0:T(2,128)} %bitcast.7, s32[3]{0:T(128)} %par_hbm.1, s32[23]{0:T(128)} %acc_hbm.1), custom_call_target="tpu_custom_call" | custom-call | tf_op jit(solution)/shard_map/pallas_call | solution.py:385
  54.2 0.8 %copy.7 = f32[2,24,3,1024]{3,1,2,0:T(8,128)} copy(f32[2,24,3,1024]{3,1,2,0:T(8,128)S(1)} %bitcast.5) | data formatting | bytes 1179648
  55.0 0.5 slice_bitcast_fusion
